TPU v7x, 32 devices: a whole 2x2x4 slice. The times are simulated.
32 devices in a mesh: groups: 2 (over y), expert: 4 (over z), hidden: 4 (over x, core).
Axes of the slice: x: 2, y: 2, z: 4, core: 2. Of those that a mesh axis runs over, the one named last changes fastest.
Arguments:
- tokens: bfloat16 [512, 4096], P(('groups', 'expert'), 'hidden'), parts along dimension 0, may hold values from -6 to 6
- norm_gain: bfloat16 [4096], P('hidden'), may hold values from 0.25 to 1.75
- gate_proj: bfloat16 [64, 768, 4096], P('expert', 'hidden'), may hold values from -0.09375 to 0.09375
- up_proj: bfloat16 [64, 768, 4096], P('expert', 'hidden'), may hold values from -0.09375 to 0.09375
- down_proj: bfloat16 [64, 768, 4096], P('expert', 'hidden'), may hold values from -0.21875 to 0.21875
- expert_ids: int32 [512, 8], P(('groups', 'expert')), parts along dimension 0, may hold values from 0 to 63, as said below
- slot_ids: int32 [512, 8], P(('groups', 'expert')), parts along dimension 0, may hold values from 0 to 11, as said below
- gate_num: int32 [512, 8], P(('groups', 'expert')), parts along dimension 0, may hold values from 1 to 255
Outputs:
- layer_out: bfloat16 [512, 4096], P(('groups', 'expert'), 'hidden'), parts along dimension 0
There are 2 independent parts, one for each index of `groups`. A program takes and returns all parts, laid end to end along the dimension named above; an argument that names none is the same for every part. Nothing has to cross between parts.
Inputs may be any that keep to these rules, and one draw needn't show every extreme that they name: `expert_ids`: each token names 8 different experts. In every aligned block of 64 tokens (the tokens of one index of the expert axis), a quarter of the experts are named by exactly 12 tokens, a quarter by 8 and the other half by 6; some expert is named by 12 tokens in every block. `slot_ids`: within an aligned block of 64 tokens, the routes that name one expert carry the slots 0 up to their count minus 1, each once.
All inputs are finite; a program needn't handle non-finite values.
Results may differ from a plain program's by a relative error of at most 0.0085.
Values may be sent and summed in bfloat16 or wider, within the bound.
A program may use at most 128 MiB of HBM per device.

v0:
```python
import jax
import jax.numpy as jnp
from jax import lax
from jax.sharding import PartitionSpec as P

D = 4096
SPECIALIST_COUNT = 64
CAP = 12
gate_scale = 1.0 / 1024.0


def route_tables(expert_ids, slot_ids, gate_num):
    slot_index = expert_ids * CAP + slot_ids
    columns = lax.broadcasted_iota(jnp.int32, (1, 1, SPECIALIST_COUNT * CAP), 2)
    matches = slot_index[:, :, None] == columns
    placing = jnp.any(matches, axis=1).astype(jnp.bfloat16)
    scaled = gate_num.astype(jnp.float32) * gate_scale
    weights = jnp.sum(jnp.where(matches, scaled[:, :, None], 0.0), axis=1).astype(jnp.bfloat16)
    return (placing, weights)


def normalize(features, gain, total_squares):
    scale = lax.rsqrt(total_squares / D + 0.5)
    return (
        features.astype(jnp.float32) * scale[:, None] * gain.astype(jnp.float32)[None, :]
    ).astype(jnp.bfloat16)


def place_rows(placing, normed, sources):
    outgoing = lax.dot_general(
        placing, normed, (((0,), (0,)), ((), ())), preferred_element_type=jnp.float32
    )
    return outgoing.astype(jnp.bfloat16).reshape(sources, -1, CAP, normed.shape[1])


def on_device(tokens, norm_gain, gate_proj, up_proj, down_proj, expert_ids, slot_ids, gate_num):
    sources = lax.axis_size("expert")
    placing, weights = route_tables(expert_ids, slot_ids, gate_num)
    local_squares = jnp.sum(jnp.square(tokens.astype(jnp.float32)), axis=1)
    squares = lax.psum(local_squares, "hidden")
    normed = normalize(tokens, norm_gain, squares)
    outgoing = place_rows(placing, normed, sources)
    received = lax.all_to_all(outgoing, "expert", split_axis=0, concat_axis=2, tiled=True)[0]
    block_cols = lax.all_gather(received, "hidden", axis=2, tiled=True)
    gate_more = jnp.einsum(
        "ehd,erd->ehr", gate_proj, block_cols, preferred_element_type=jnp.float32
    )
    up_more = jnp.einsum("ehd,erd->ehr", up_proj, block_cols, preferred_element_type=jnp.float32)
    activated = (jax.nn.silu(gate_more) * up_more).astype(jnp.bfloat16)
    partial_value = jnp.einsum(
        "ehr,ehd->erd", activated, down_proj, preferred_element_type=jnp.float32
    ).astype(jnp.bfloat16)
    returned = lax.all_to_all(
        partial_value[None], "expert", split_axis=2, concat_axis=0, tiled=True
    )
    returned = returned.reshape(-1, returned.shape[-1])
    partial_out = jnp.dot(weights, returned, preferred_element_type=jnp.float32)
    return lax.psum_scatter(partial_out, "hidden", scatter_dimension=1, tiled=True).astype(
        jnp.bfloat16
    )


def solution(mesh):
    placed = (
        P(("groups", "expert"), "hidden"),
        P("hidden"),
        P("expert", "hidden", None),
        P("expert", "hidden", None),
        P("expert", "hidden", None),
        P(("groups", "expert"), None),
        P(("groups", "expert"), None),
        P(("groups", "expert"), None),
    )
    return jax.shard_map(
        on_device,
        mesh=mesh,
        in_specs=placed,
        out_specs=P(("groups", "expert"), "hidden"),
        check_vma=False,
    )
```

profile of v0, /device:TPU:0, one launch (start us, length us, event | category | flops | bytes accessed | tf_op | source)
XLA Modules:
  0.0 358.5 jit_solution(16859934131630568120)
XLA Ops:
  6.5 0.0 all-gather.2.cloned.1.call-start
  6.5 0.7 multiply_add_fusion
  7.2 0.1 copy.24
  7.3 0.5 fusion.1
  7.9 0.7 convert_element_type.32
  8.6 1.0 fusion.10
  9.6 8.4 %psum.7 = f32[64]{0:T(128)S(1)} all-reduce(f32[64]{0:T(128)S(1)} %fusion.10), channel_id=1, replica_groups=mesh['groups'=2,'expert'=4,'hidden'=4] {'hidden'}, use_global_device_ids=true, to_apply=%region_3.4 | all-reduce | flops 64 | bytes 512 | tf_op jit(solution)/shard_map/psum | solution.py:40
  18.0 2.7 convolution_convert_fusion.1
  20.7 2.4 reshape.12
  23.1 0.9 copy.26
  23.9 40.4 %all_to_all.30 = bf16[4,16,12,1024]{3,1,2,0:T(8,128)(2,1)S(1)} all-to-all(bf16[4,16,12,1024]{3,1,2,0:T(8,128)(2,1)S(1)} %copy.26), channel_id=1, replica_groups=mesh['groups'=2,'expert'=4,'hidden'=4] {'expert'}, dimensions={0} | all-to-all | bytes 3145728 | tf_op jit(solution)/shard_map/all_to_all | solution.py:43
  64.4 2.0 copy.27
  66.4 0.0 all-gather.2.cloned.1.call-update
  66.4 45.7 %all-gather.2.cloned.1.call-done = bf16[16,48,4096]{2,1,0:T(8,128)(2,1)} async-done(((bf16[16,48,1024]{2,1,0:T(8,128)(2,1)}), bf16[16,48,4096]{2,1,0:T(8,128)(2,1)}) %all-gather.2.cloned.1.call-update) | async-done | bytes 6291472 | tf_op jit(solution)/shard_map/all_gather | solution.py:44
  112.0 14.1 %convolution_bitcast_fusion.1 = f32[16,192,48]{1,2,0:T(8,128)S(1)} fusion(bf16[16,48,4096]{2,1,0:T(8,128)(2,1)} %all-gather.2.cloned.1.call-done, bf16[16,192,4096]{2,1,0:T(8,128)(2,1)} %param.10), kind=kOutput, calls=%fused_computation.7 | convolution fusion | flops 1207959552 | bytes 32047104 | tf_op jit(solution)/shard_map/ehd,erd->ehr/dot_general | solution.py:45
  126.2 22.9 %fusion = bf16[1,16,48,4096]{3,2,1,0:T(8,128)(2,1)} fusion(bf16[16,192,4096]{2,1,0:T(8,128)(2,1)} %param.12, bf16[16,48,4096]{2,1,0:T(8,128)(2,1)} %all-gather.2.cloned.1.call-done, bf16[16,192,4096]{2,1,0:T(8,128)(2,1)} %param.11, f32[16,192,48]{1,2,0:T(8,128)S(1)} %convolution_bitcast_fusion.1), kind=kOutput, calls=%fused_computation.1 | convolution fusion | flops 2419949568 | bytes 63504384 | tf_op jit(solution)/shard_map/ehr,ehd->erd/dot_general | solution.py:50
  149.1 8.9 %copy.28 = bf16[1,16,48,4096]{3,1,0,2:T(8,128)(2,1)} copy(bf16[1,16,48,4096]{3,2,1,0:T(8,128)(2,1)} %fusion) | data formatting | bytes 12582912 | tf_op jit(solution)/shard_map/broadcast_in_dim | solution.py:54
  158.0 0.0 copy-start
  158.0 5.4 %all-to-all-start.1 = ((bf16[1,16,48,4096]{3,1,0,2:T(8,128)(2,1)}), bf16[1,16,48,4096]{3,1,0,2:T(8,128)(2,1)}, u32[]{:S(2)}, u32[]{:S(2)}) async-start(bf16[1,16,48,4096]{3,1,0,2:T(8,128)(2,1)} %copy.28), calls=%async_computation.1 | async-start | bytes 12582912 | tf_op jit(solution)/shard_map/all_to_all | solution.py:53
  163.5 0.3 reduce-scatter.2.cloned.1.call-start
  163.7 0.0 copy-done
  163.7 0.1 copy.25
  163.8 0.6 select_reduce_fusion
  164.4 137.9 %all-to-all-done.1 = bf16[1,16,48,4096]{3,1,0,2:T(8,128)(2,1)} async-done(((bf16[1,16,48,4096]{3,1,0,2:T(8,128)(2,1)}), bf16[1,16,48,4096]{3,1,0,2:T(8,128)(2,1)}, u32[]{:S(2)}, u32[]{:S(2)}) %all-to-all-start.1) | async-done | bytes 6291488 | tf_op jit(solution)/shard_map/all_to_all | solution.py:53
  302.3 9.8 %copy.29 = bf16[4,1,16,12,4096]{4,3,2,0,1:T(8,128)(2,1)} copy(bf16[4,1,16,12,4096]{4,2,3,0,1:T(8,128)(2,1)} %bitcast.7) | data formatting | bytes 12582912 | tf_op jit(solution)/shard_map/all_to_all | solution.py:53
  312.1 9.9 %reshape.13 = bf16[768,4096]{1,0:T(8,128)(2,1)} reshape(bf16[4,1,16,12,4096]{4,3,2,0,1:T(8,128)(2,1)} %copy.29) | data formatting | bytes 12582912 | tf_op jit(solution)/shard_map/reshape | solution.py:56
  322.0 5.0 %fusion.19 = f32[64,4096]{1,0:T(8,128)} fusion(bf16[64,768]{1,0:T(8,128)(2,1)S(1)} %select_reduce_fusion, bf16[768,4096]{1,0:T(8,128)(2,1)} %reshape.13), kind=kOutput, calls=%fused_computation.29 | convolution fusion | flops 402653184 | bytes 7438336 | tf_op jit(solution)/shard_map/dot_general | solution.py:57
  327.0 0.0 reduce-scatter.2.cloned.1.call-update
  327.0 23.0 %reduce-scatter.2.cloned.1.call-done = f32[64,1024]{1,0:T(8,128)} async-done(((f32[64,4096]{1,0:T(8,128)}), f32[64,1024]{1,0:T(8,128)}) %reduce-scatter.2.cloned.1.call-update) | async-done | bytes 262160 | tf_op jit(solution)/shard_map/reduce_scatter | solution.py:58
  350.0 1.6 convert_element_type.37
  (2 shorter events, 0.0 us)
Async XLA Ops:
  6.5 105.5 %all-gather.2.cloned.1.call-start = ((), (), s32[]{:S(2)}) async-start(), calls=%async_computation.3 | async-start | bytes 7864320 | tf_op jit(solution)/shard_map/all_gather | solution.py:44
  158.0 5.7 %copy-start = (s32[64,8]{0,1:T(8,128)S(1)}, s32[64,8]{0,1:T(8,128)}, u32[]{:S(2)}) copy-start(s32[64,8]{0,1:T(8,128)} %param.15) | copy-start | bytes 6148
  158.0 144.3 %all-to-all-start.1 = ((bf16[1,16,48,4096]{3,1,0,2:T(8,128)(2,1)}), bf16[1,16,48,4096]{3,1,0,2:T(8,128)(2,1)}, u32[]{:S(2)}, u32[]{:S(2)}) async-start(bf16[1,16,48,4096]{3,1,0,2:T(8,128)(2,1)} %copy.28), calls=%async_computation.1 | async-start | bytes 12582912 | tf_op jit(solution)/shard_map/all_to_all | solution.py:53
  163.5 186.6 %reduce-scatter.2.cloned.1.call-start = ((), (), s32[]{:S(2)}) async-start(), calls=%async_computation.4 | async-start | bytes 1310720 | tf_op jit(solution)/shard_map/reduce_scatter | solution.py:58
Sparse Core Ops, SparseCore 0:
  66.5 45.4 all-gather.1
  327.1 22.8 reduce-scatter.1
where the time goes:
time: 359 us; the launch traced here: 358 us
  waiting for transfers between devices  207 us (58%)
  blocking collectives  48.8 us (14%)
  matrix products  44.7 us (12%)
  local copies, waits for them, and re-layouts  34 us (9%)
  between operations  13.5 us (4%)
  starting transfers between devices  5.71 us (2%)
  other arithmetic  5.15 us (1%)
    all_to_all x1, waiting for transfers between devices, on_device(): lax.all_to_all(partial_value[None], 'expert', split_axis=2, concat_axis=0...  138 us
    all_gather x1, waiting for transfers between devices, on_device(): block_cols = lax.all_gather(received, 'hidden', axis=2, tiled=True)  45.7 us
    all_to_all x1, blocking collectives, on_device(): lax.all_to_all(outgoing, 'expert', split_axis=0, concat_axis=2, tiled=True)  40.4 us
    reduce_scatter x1, waiting for transfers between devices, on_device(): lax.psum_scatter(partial_out, 'hidden', scatter_dimension=1, tiled=True)  23 us
    dot_general x1, matrix products, on_device(): jnp.einsum('ehr,ehd->erd', activated, down_proj, preferred_element_type=j...  22.9 us
    dot_general x1, matrix products, on_device(): jnp.einsum('ehd,erd->ehr', gate_proj, block_cols, preferred_element_type=...  14.1 us
    reshape x1, local copies, waits for them, and re-layouts, on_device(): returned = returned.reshape(-1, returned.shape[-1])  9.85 us
    all_to_all x1, local copies, waits for them, and re-layouts, on_device(): lax.all_to_all(partial_value[None], 'expert', split_axis=2, concat_axis=0...  9.84 us
  transfers between devices with their start and end apart: 3, of which 3 were waited for; matrix products, arithmetic and copies ran while one was open for 0% of the time, Pallas kernels for 0%

commit v1 on v0

--- a/solution.py
+++ b/solution.py
@@ -41,7 +41,9 @@
     normed = normalize(tokens, norm_gain, squares)
     outgoing = place_rows(placing, normed, sources)
     received = lax.all_to_all(outgoing, "expert", split_axis=0, concat_axis=2, tiled=True)[0]
-    block_cols = lax.all_gather(received, "hidden", axis=2, tiled=True)
+    block_cols = jnp.concatenate(
+        lax.all_to_all(jnp.stack([received] * lax.axis_size("hidden")), "hidden", 0, 0), axis=2
+    )
     gate_more = jnp.einsum(
         "ehd,erd->ehr", gate_proj, block_cols, preferred_element_type=jnp.float32
     )

time: 359 us -> 389 us (1.084)
  blocking collectives: 48.8 us -> 122 us
  waiting for transfers between devices: 207 us -> 160 us
    all_to_all x0 -> x1, blocking collectives: none -> 73.3 us  [on_device(): lax.all_to_all(jnp.stack([received] * lax.axis_size('hidden')), 'hidden',...]
    all_gather x1 -> x0, waiting for transfers between devices: 45.7 us -> none  [on_device(): block_cols = lax.all_gather(received, 'hidden', axis=2, tiled=True)]
  transfers between devices with their start and end apart: 3 -> 2, of which waited for: 3 -> 2; matrix products, arithmetic and copies ran while one was open for 0% -> 0% of each run, Pallas kernels for 0% -> 0%
where the time goes in v1:
time: 389 us; the launch traced here: 388 us
  waiting for transfers between devices  160 us (41%)
  blocking collectives  122 us (31%)
  matrix products  44.8 us (12%)
  local copies, waits for them, and re-layouts  37 us (10%)
  between operations  13.5 us (3%)
  starting transfers between devices  5.71 us (1%)
  other arithmetic  5.15 us (1%)
    all_to_all x1, waiting for transfers between devices, on_device(): lax.all_to_all(partial_value[None], 'expert', split_axis=2, concat_axis=0...  137 us
    all_to_all x1, blocking collectives, on_device(): lax.all_to_all(jnp.stack([received] * lax.axis_size('hidden')), 'hidden',...  73.3 us
    all_to_all x1, blocking collectives, on_device(): lax.all_to_all(outgoing, 'expert', split_axis=0, concat_axis=2, tiled=True)  40.4 us
    reduce_scatter x1, waiting for transfers between devices, on_device(): lax.psum_scatter(partial_out, 'hidden', scatter_dimension=1, tiled=True)  23.2 us
    dot_general x1, matrix products, on_device(): jnp.einsum('ehr,ehd->erd', activated, down_proj, preferred_element_type=j...  23 us
    dot_general x1, matrix products, on_device(): jnp.einsum('ehd,erd->ehr', gate_proj, block_cols, preferred_element_type=...  14.1 us
    reshape x1, local copies, waits for them, and re-layouts, on_device(): returned = returned.reshape(-1, returned.shape[-1])  9.85 us
    all_to_all x1, local copies, waits for them, and re-layouts, on_device(): lax.all_to_all(partial_value[None], 'expert', split_axis=2, concat_axis=0...  9.84 us
  transfers between devices with their start and end apart: 2, of which 2 were waited for; matrix products, arithmetic and copies ran while one was open for 0% of the time, Pallas kernels for 0%

profile of v1, /device:TPU:0, one launch (start us, length us, event | category | flops | bytes accessed | tf_op | source)
XLA Modules:
  0.0 388.4 jit_solution(17168114448860215463)
XLA Ops:
  6.5 0.7 multiply_add_fusion
  7.2 0.1 copy.24
  7.3 0.5 fusion.1
  7.9 0.7 convert_element_type.32
  8.6 1.0 fusion.10
  9.6 8.4 %psum.7 = f32[64]{0:T(128)S(1)} all-reduce(f32[64]{0:T(128)S(1)} %fusion.10), channel_id=1, replica_groups=mesh['groups'=2,'expert'=4,'hidden'=4] {'hidden'}, use_global_device_ids=true, to_apply=%region_3.4 | all-reduce | flops 64 | bytes 512 | tf_op jit(solution)/shard_map/psum | solution.py:40
  18.0 2.7 convolution_convert_fusion.1
  20.7 2.4 reshape.19
  23.1 0.9 copy.26
  23.9 40.4 %all_to_all.38 = bf16[4,16,12,1024]{3,1,2,0:T(8,128)(2,1)S(1)} all-to-all(bf16[4,16,12,1024]{3,1,2,0:T(8,128)(2,1)S(1)} %copy.26), channel_id=1, replica_groups=mesh['groups'=2,'expert'=4,'hidden'=4] {'expert'}, dimensions={0} | all-to-all | bytes 3145728 | tf_op jit(solution)/shard_map/all_to_all | solution.py:43
  64.4 0.9 copy.27
  65.2 0.9 stack.3
  66.1 73.3 %all_to_all.39 = bf16[4,16,48,1024]{3,2,1,0:T(8,128)(2,1)S(1)} all-to-all(bf16[4,16,48,1024]{3,2,1,0:T(8,128)(2,1)S(1)} %stack.3), channel_id=1, replica_groups=mesh['groups'=2,'expert'=4,'hidden'=4] {'hidden'}, dimensions={0} | all-to-all | bytes 12582912 | tf_op jit(solution)/shard_map/all_to_all | solution.py:45
  139.4 3.4 copy.31
  142.7 14.1 %convolution_bitcast_fusion.1 = f32[16,192,48]{1,2,0:T(8,128)S(1)} fusion(bf16[16,48,4096]{2,1,0:T(8,128)(2,1)} %bitcast.33, bf16[16,192,4096]{2,1,0:T(8,128)(2,1)} %param.10), kind=kOutput, calls=%fused_computation.7 | convolution fusion | flops 1207959552 | bytes 32047104 | tf_op jit(solution)/shard_map/ehd,erd->ehr/dot_general | solution.py:47
  156.9 23.0 %fusion = bf16[1,16,48,4096]{3,2,1,0:T(8,128)(2,1)} fusion(bf16[16,192,4096]{2,1,0:T(8,128)(2,1)} %param.12, bf16[16,48,4096]{2,1,0:T(8,128)(2,1)} %bitcast.34, bf16[16,192,4096]{2,1,0:T(8,128)(2,1)} %param.11, f32[16,192,48]{1,2,0:T(8,128)S(1)} %convolution_bitcast_fusion.1), kind=kOutput, calls=%fused_computation.1 | convolution fusion | flops 2419949568 | bytes 63504384 | tf_op jit(solution)/shard_map/ehr,ehd->erd/dot_general | solution.py:52
  179.8 8.8 %copy.29 = bf16[1,16,48,4096]{3,1,0,2:T(8,128)(2,1)} copy(bf16[1,16,48,4096]{3,2,1,0:T(8,128)(2,1)} %fusion) | data formatting | bytes 12582912 | tf_op jit(solution)/shard_map/broadcast_in_dim | solution.py:56
  188.6 0.0 copy-start
  188.6 5.4 %all-to-all-start.2 = ((bf16[1,16,48,4096]{3,1,0,2:T(8,128)(2,1)}), bf16[1,16,48,4096]{3,1,0,2:T(8,128)(2,1)}, u32[]{:S(2)}, u32[]{:S(2)}) async-start(bf16[1,16,48,4096]{3,1,0,2:T(8,128)(2,1)} %copy.29), calls=%async_computation.2 | async-start | bytes 12582912 | tf_op jit(solution)/shard_map/all_to_all | solution.py:55
  194.1 0.3 reduce-scatter.2.cloned.1.call-start
  194.3 0.0 copy-done
  194.4 0.1 copy.25
  194.4 0.6 select_reduce_fusion
  195.0 137.1 %all-to-all-done.2 = bf16[1,16,48,4096]{3,1,0,2:T(8,128)(2,1)} async-done(((bf16[1,16,48,4096]{3,1,0,2:T(8,128)(2,1)}), bf16[1,16,48,4096]{3,1,0,2:T(8,128)(2,1)}, u32[]{:S(2)}, u32[]{:S(2)}) %all-to-all-start.2) | async-done | bytes 6291488 | tf_op jit(solution)/shard_map/all_to_all | solution.py:55
  332.1 9.8 %copy.30 = bf16[4,1,16,12,4096]{4,3,2,0,1:T(8,128)(2,1)} copy(bf16[4,1,16,12,4096]{4,2,3,0,1:T(8,128)(2,1)} %bitcast.8) | data formatting | bytes 12582912 | tf_op jit(solution)/shard_map/all_to_all | solution.py:55
  342.0 9.9 %reshape.22 = bf16[768,4096]{1,0:T(8,128)(2,1)} reshape(bf16[4,1,16,12,4096]{4,3,2,0,1:T(8,128)(2,1)} %copy.30) | data formatting | bytes 12582912 | tf_op jit(solution)/shard_map/reshape | solution.py:58
  351.8 5.0 %fusion.19 = f32[64,4096]{1,0:T(8,128)} fusion(bf16[64,768]{1,0:T(8,128)(2,1)S(1)} %select_reduce_fusion, bf16[768,4096]{1,0:T(8,128)(2,1)} %reshape.22), kind=kOutput, calls=%fused_computation.29 | convolution fusion | flops 402653184 | bytes 7438336 | tf_op jit(solution)/shard_map/dot_general | solution.py:59
  356.8 0.0 reduce-scatter.2.cloned.1.call-update
  356.8 23.2 %reduce-scatter.2.cloned.1.call-done = f32[64,1024]{1,0:T(8,128)} async-done(((f32[64,4096]{1,0:T(8,128)}), f32[64,1024]{1,0:T(8,128)}) %reduce-scatter.2.cloned.1.call-update) | async-done | bytes 262160 | tf_op jit(solution)/shard_map/reduce_scatter | solution.py:60
  380.0 1.6 convert_element_type.37
  (2 shorter events, 0.0 us)
Async XLA Ops:
  188.6 5.7 %copy-start = (s32[64,8]{0,1:T(8,128)S(1)}, s32[64,8]{0,1:T(8,128)}, u32[]{:S(2)}) copy-start(s32[64,8]{0,1:T(8,128)} %param.15) | copy-start | bytes 6148
  188.6 143.5 %all-to-all-start.2 = ((bf16[1,16,48,4096]{3,1,0,2:T(8,128)(2,1)}), bf16[1,16,48,4096]{3,1,0,2:T(8,128)(2,1)}, u32[]{:S(2)}, u32[]{:S(2)}) async-start(bf16[1,16,48,4096]{3,1,0,2:T(8,128)(2,1)} %copy.29), calls=%async_computation.2 | async-start | bytes 12582912 | tf_op jit(solution)/shard_map/all_to_all | solution.py:55
  194.1 185.9 %reduce-scatter.2.cloned.1.call-start = ((), (), s32[]{:S(2)}) async-start(), calls=%async_computation.4 | async-start | bytes 1310720 | tf_op jit(solution)/shard_map/reduce_scatter | solution.py:60
Sparse Core Ops, SparseCore 0:
  356.9 22.9 reduce-scatter.1
